TPU v7x, 128 devices: a whole 4x4x4 slice. The times are simulated.
128 devices in a mesh: dp: 8 (over z, core), cp: 16 (over x, y).
Axes of the slice: x: 4, y: 4, z: 4, core: 2. Of those that a mesh axis runs over, the one named last changes fastest.
Arguments:
- row_owner: int32 [16384, 1], P(('dp', 'cp')), may hold values from 0 to 127; in each aligned block of 128 rows (0 to 127, 128 to 255, ...) at most 4 rows name the same one
- slot_row: int32 [16384], P(('dp', 'cp')), may hold values from 0 to 2559
- hot_table: bfloat16 [65536, 512], P(('dp', 'cp')), may hold values from -6 to 6
- cold_table: bfloat16 [262144, 128], P(('dp', 'cp')), may hold values from -6 to 6
- cold_projection: bfloat16 [128, 512], replicated, may hold values from -0.5 to 0.5
- joined_weight: bfloat16 [512, 2048], replicated, may hold values from -0.25 to 0.25
- output_weight: bfloat16 [512, 512], replicated, may hold values from -0.25 to 0.25
- cotangent: bfloat16 [16384, 512], P(('dp', 'cp')), may hold values from -6 to 6
Outputs:
- layer_out: bfloat16 [16384, 512], P(('dp', 'cp'))
- hot_gradient: float32 [65536, 512], P(('dp', 'cp'))
- cold_gradient: float32 [262144, 128], P(('dp', 'cp'))
- projection_gradient: float32 [128, 512], replicated
- joined_gradient: float32 [512, 2048], replicated
- output_gradient: float32 [512, 512], replicated
Inputs may be any that keep to these rules, and one draw needn't show every extreme that they name: `row_owner`: in each aligned block of 128 rows (the rows of one device) no owner is named by more than 4 rows.
All inputs are finite; a program needn't handle non-finite values.
Results may differ from a plain program's by a relative error of at most 0.013.
Values may be sent and summed in bfloat16 or wider, within the bound.
A program may use at most 128 MiB of HBM per device.

v0:
```python
import math
import jax
import jax.numpy as jnp
from jax import lax
from jax.sharding import PartitionSpec as P

HEADS = 8
EPSILON = 1e-05
block_limit = 1024


def side_by_side(arrays, axis, dim, along):
    ends, at = ([], 0)
    for a in arrays[:-1]:
        at += a.shape[along]
        ends.append(at)
    both = jnp.concatenate(arrays, axis=along)
    return tuple(jnp.split(lax.all_gather(both, axis, axis=dim, tiled=True), ends, axis=along))


def cut_along(x, dim, length):
    dims = x.shape
    blocks = x.reshape(*dims[:dim], length, dims[dim] // length, *dims[dim + 1 :])
    return jnp.moveaxis(blocks, dim, 0)


def edges_of(length, count):
    unit = 8 if length >= 8 * count else 1
    return [length // unit * k // count * unit for k in range(1, count)]


def in_order(blocks, dim):
    blocks = jnp.moveaxis(blocks, 0, dim)
    dims = blocks.shape
    return blocks.reshape(*dims[:dim], dims[dim] * dims[dim + 1], *dims[dim + 2 :])


def several_exchanges(x, axis, pieces, split_dim, concat_dim):
    blocks = cut_along(x, split_dim, lax.axis_size(axis))
    split_at = max(range(1, max(2, blocks.ndim - 1)), key=lambda d: blocks.shape[d])
    gathered = []
    for piece in jnp.split(blocks, edges_of(blocks.shape[split_at], pieces), axis=split_at):
        if piece.size:
            gathered.append(lax.all_to_all(piece, axis, split_axis=0, concat_axis=0, tiled=True))
    return in_order(jnp.concatenate(gathered, axis=split_at), concat_dim)


def silu_slope(values):
    sigmoid_v = jax.nn.sigmoid(values)
    return sigmoid_v * (1.0 + values * (1.0 - sigmoid_v))


def layer_normalize(values):
    average = jnp.mean(values, axis=-1, keepdims=True)
    centred = values - average
    inverse = lax.rsqrt(jnp.mean(centred * centred, axis=-1, keepdims=True) + EPSILON)
    return (centred * inverse, inverse)


def normalize_back(gradient, normed, inverse):
    first_term = jnp.mean(gradient, axis=-1, keepdims=True)
    second_term = jnp.mean(gradient * normed, axis=-1, keepdims=True)
    return (gradient - first_term - normed * second_term) * inverse


def masked_scores(query_heads, key_heads, query_index, key_index, score_scale):
    scores = (
        jnp.einsum("qhd,khd->hqk", query_heads, key_heads, preferred_element_type=jnp.float32)
        * score_scale
    )
    allowed = (key_index[None, :] <= query_index[:, None])[None]
    weights = jnp.where(allowed, jax.nn.silu(scores), 0.0).astype(jnp.bfloat16)
    return (scores, allowed, weights)


def score_deltas(
    query_heads, key_heads, value_heads, delta_heads, query_index, key_index, score_scale
):
    scores, allowed, weights = masked_scores(
        query_heads, key_heads, query_index, key_index, score_scale
    )
    delta_weights = jnp.einsum(
        "qhd,khd->hqk", delta_heads, value_heads, preferred_element_type=jnp.float32
    )
    delta_scores = jnp.where(allowed, delta_weights * silu_slope(scores) * score_scale, 0.0).astype(
        jnp.bfloat16
    )
    return (weights, delta_scores)


def local(
    row_owner,
    slot_row,
    hot_table,
    cold_table,
    cold_projection,
    joined_weight,
    output_weight,
    cotangent,
):
    tokens_here = slot_row.shape[0]
    model_width = output_weight.shape[0]
    hot_count = hot_table.shape[0]
    cold_count = cold_table.shape[0]
    cold_width = cold_table.shape[1]
    head_count = HEADS
    head_size = model_width // head_count
    score_scale = 1.0 / math.sqrt(head_size)
    devices = lax.axis_size(("dp", "cp"))
    group_index = lax.axis_index("cp")
    capacity = 2 * tokens_here // devices + 2
    owners = row_owner[:, 0]
    is_hot = slot_row < hot_count
    is_cold = jnp.logical_not(is_hot)
    onehot = (owners[:, None] == jnp.arange(devices, dtype=jnp.int32)[None, :]).astype(jnp.bfloat16)
    lower_mask = (jnp.arange(tokens_here)[:, None] > jnp.arange(tokens_here)[None, :]).astype(
        jnp.bfloat16
    )
    earlier = jnp.dot(lower_mask, onehot, preferred_element_type=jnp.float32)
    rank_in_owner = jnp.sum(earlier * onehot.astype(jnp.float32), axis=1).astype(jnp.int32)
    slot_index = owners * capacity + rank_in_owner
    requests = (
        jnp.full((devices * capacity,), -1, jnp.int32)
        .at[slot_index]
        .set(slot_row)
        .reshape(devices, capacity)
    )
    asked_rows = lax.all_to_all(requests, ("dp", "cp"), split_axis=0, concat_axis=0, tiled=True)
    valid_hot = (asked_rows >= 0) & (asked_rows < hot_count)
    valid_cold = asked_rows >= hot_count
    nothing = jnp.zeros((), jnp.bfloat16)
    hot_pick = jnp.where(
        valid_hot[..., None], hot_table[jnp.clip(asked_rows, 0, hot_count - 1)], nothing
    )
    cold_pick = jnp.where(
        valid_cold[..., None],
        cold_table[jnp.clip(asked_rows - hot_count, 0, cold_count - 1)],
        nothing,
    )
    padded = jnp.pad(cold_pick, ((0, 0), (0, 0), (0, model_width - cold_width)))
    packed = jnp.where(valid_hot[..., None], hot_pick, padded)
    returned = lax.all_to_all(packed, ("dp", "cp"), split_axis=0, concat_axis=0, tiled=True)
    fetched = returned.reshape(devices * capacity, model_width)[slot_index]
    cold_vector = fetched[:, :cold_width]
    cold_embed = jnp.dot(cold_vector, cold_projection, preferred_element_type=jnp.float32)
    embedded = jnp.where(is_hot[:, None], fetched.astype(jnp.float32), cold_embed)
    normed, inverse = layer_normalize(embedded)
    normed_low = normed.astype(jnp.bfloat16)
    hidden = jnp.dot(normed_low, joined_weight, preferred_element_type=jnp.float32)
    active = jax.nn.silu(hidden).astype(jnp.bfloat16)
    gate_part = active[:, :model_width]
    attention_rows = active[:, model_width:]
    segments = [(0, tokens_here, group_index * tokens_here)]
    value_rows = attention_rows[:, :model_width]
    query_rows = attention_rows[:, model_width : 2 * model_width]
    key_rows = attention_rows[:, 2 * model_width :]
    local_index = jnp.concatenate(
        [first + jnp.arange(count, dtype=jnp.int32) for start, count, first in segments]
    )
    all_keys, all_values = side_by_side((key_rows, value_rows), "cp", 0, 1)
    length = all_keys.shape[0]
    key_span = min(length, block_limit)
    heads_shape = (tokens_here, head_count, head_size)
    query_heads = query_rows.reshape(heads_shape)

    def key_slices(counter):
        offset = counter * key_span
        key_block = lax.dynamic_slice_in_dim(all_keys, offset, key_span, 0).reshape(
            key_span, head_count, head_size
        )
        value_block = lax.dynamic_slice_in_dim(all_values, offset, key_span, 0).reshape(
            key_span, head_count, head_size
        )
        key_index = offset + jnp.arange(key_span, dtype=jnp.int32)
        return (offset, key_block, value_block, key_index)

    def blocks_needed(first, count):
        return (first + count + key_span - 1) // key_span

    start, count, first = segments[0]
    segment_queries = query_heads
    segment_index = first + jnp.arange(count, dtype=jnp.int32)

    def forward_step(
        counter, running, segment_queries=segment_queries, segment_index=segment_index
    ):
        offset, key_block, value_block, key_index = key_slices(counter)
        scores, allowed, weights = masked_scores(
            segment_queries, key_block, segment_index, key_index, score_scale
        )
        return running + jnp.einsum(
            "hqk,khd->qhd", weights, value_block, preferred_element_type=jnp.float32
        )

    empty_part = jnp.zeros((count, head_count, head_size), jnp.float32)
    attended_parts = lax.fori_loop(0, blocks_needed(first, count), forward_step, empty_part)
    attended = attended_parts.reshape(tokens_here, model_width)
    mixed, inverse_mix = layer_normalize(attended)
    gated = (mixed * gate_part.astype(jnp.float32)).astype(jnp.bfloat16)
    branch = jnp.dot(gated, output_weight, preferred_element_type=jnp.float32)
    layer_out = (embedded + branch).astype(jnp.bfloat16)
    delta_gated = jnp.dot(cotangent, output_weight.T, preferred_element_type=jnp.float32)
    delta_gate = delta_gated * mixed
    delta_attended = normalize_back(
        delta_gated * gate_part.astype(jnp.float32), mixed, inverse_mix
    ).astype(jnp.bfloat16)
    delta_heads = delta_attended.reshape(heads_shape)
    empty_heads = jnp.zeros(heads_shape, jnp.float32)
    start, count, first = segments[0]
    segment_queries = query_heads
    segment_deltas = delta_heads
    segment_index = first + jnp.arange(count, dtype=jnp.int32)

    def query_step(
        counter,
        running,
        segment_queries=segment_queries,
        segment_deltas=segment_deltas,
        segment_index=segment_index,
    ):
        offset, key_block, value_block, key_index = key_slices(counter)
        weights, delta_scores = score_deltas(
            segment_queries,
            key_block,
            value_block,
            segment_deltas,
            segment_index,
            key_index,
            score_scale,
        )
        return running + jnp.einsum(
            "hqk,khd->qhd", delta_scores, key_block, preferred_element_type=jnp.float32
        )

    empty_part = jnp.zeros((count, head_count, head_size), jnp.float32)
    query_parts = lax.fori_loop(0, blocks_needed(first, count), query_step, empty_part)
    key_heads = key_rows.reshape(heads_shape)
    value_heads = value_rows.reshape(heads_shape)
    key_lowest = jnp.min(local_index)
    query_piece, delta_piece = side_by_side((query_rows, delta_attended), "cp", 0, 1)
    row_count = query_piece.shape[0]
    sub_rows = math.gcd(row_count, block_limit)

    def inner_step(counter, partial_sums):
        start_row = counter * sub_rows
        query_block = lax.dynamic_slice_in_dim(query_piece, start_row, sub_rows, 0).reshape(
            sub_rows, head_count, head_size
        )
        delta_block = lax.dynamic_slice_in_dim(delta_piece, start_row, sub_rows, 0).reshape(
            sub_rows, head_count, head_size
        )
        query_index = start_row + jnp.arange(sub_rows, dtype=jnp.int32)

        def accumulate(sums_in):
            weights, delta_scores = score_deltas(
                query_block,
                key_heads,
                value_heads,
                delta_block,
                query_index,
                local_index,
                score_scale,
            )
            key_sum = sums_in[0] + jnp.einsum(
                "hqk,qhd->khd", delta_scores, query_block, preferred_element_type=jnp.float32
            )
            value_sum = sums_in[1] + jnp.einsum(
                "hqk,qhd->khd", weights, delta_block, preferred_element_type=jnp.float32
            )
            return (key_sum, value_sum)

        return lax.cond(
            jnp.max(query_index) >= key_lowest, accumulate, lambda sums_in: sums_in, partial_sums
        )

    key_sum, value_sum = lax.fori_loop(
        0, row_count // sub_rows, inner_step, (empty_heads, empty_heads)
    )
    delta_key = key_sum.reshape(tokens_here, model_width)
    delta_value = value_sum.reshape(tokens_here, model_width)
    attention_grads = jnp.concatenate(
        [delta_value, query_parts.reshape(tokens_here, model_width), delta_key], axis=1
    )
    delta_active = jnp.concatenate([delta_gate, attention_grads], axis=1)
    delta_hidden = (delta_active * silu_slope(hidden)).astype(jnp.bfloat16)
    delta_normed = jnp.dot(delta_hidden, joined_weight.T, preferred_element_type=jnp.float32)
    delta_embed = normalize_back(delta_normed, normed, inverse) + cotangent.astype(jnp.float32)
    cold_float = jnp.where(is_cold[:, None], cold_vector.astype(jnp.float32), 0.0)
    joined_local = jnp.dot(normed_low.T, delta_hidden, preferred_element_type=jnp.float32)
    output_local = jnp.dot(gated.T, cotangent, preferred_element_type=jnp.float32)
    projection_local = jnp.dot(cold_float.T, delta_embed, precision=lax.Precision.HIGHEST)
    joined_sum, output_sum, projection_sum = (
        lax.psum(joined_local.astype(jnp.bfloat16), ("dp", "cp")).astype(jnp.float32),
        lax.psum(output_local.astype(jnp.bfloat16), ("dp", "cp")).astype(jnp.float32),
        lax.psum(projection_local.astype(jnp.bfloat16), ("dp", "cp")).astype(jnp.float32),
    )
    norm_scale = (tokens_here * devices) ** (-0.5)
    cold_event = jnp.where(
        is_cold[:, None],
        jnp.dot(
            delta_embed, cold_projection.astype(jnp.float32).T, precision=lax.Precision.HIGHEST
        ),
        0.0,
    )
    hot_event = jnp.where(is_hot[:, None], delta_embed, 0.0)
    padded_event = jnp.pad(cold_event, ((0, 0), (0, model_width - cold_width)))
    packed_event = jnp.where(is_hot[:, None], hot_event, padded_event)
    buffer = (
        jnp.zeros((devices * capacity, model_width), jnp.float32)
        .at[slot_index]
        .set(packed_event)
        .reshape(devices, capacity, model_width)
    )
    arrived = several_exchanges(buffer.astype(jnp.bfloat16), ("dp", "cp"), 2, 0, 0).astype(
        buffer.dtype
    )
    cold_arrived = arrived[..., :cold_width]
    hot_target = jnp.where(valid_hot, asked_rows, hot_count).reshape(-1)
    cold_target = jnp.where(valid_cold, asked_rows - hot_count, cold_count).reshape(-1)
    hot_gradient = (
        jnp.zeros((hot_count, model_width), jnp.float32)
        .at[hot_target]
        .add(arrived.reshape(-1, model_width), mode="drop")
    )
    cold_gradient = (
        jnp.zeros((cold_count, cold_width), jnp.float32)
        .at[cold_target]
        .add(cold_arrived.reshape(-1, cold_width), mode="drop")
    )
    return (
        layer_out,
        hot_gradient,
        cold_gradient,
        projection_sum * norm_scale,
        joined_sum * norm_scale,
        output_sum * norm_scale,
    )


def solution(mesh):
    placed = (
        P(("dp", "cp"), None),
        P(("dp", "cp")),
        P(("dp", "cp"), None),
        P(("dp", "cp"), None),
        P(),
        P(),
        P(),
        P(("dp", "cp"), None),
    )
    return jax.shard_map(
        local,
        mesh=mesh,
        in_specs=placed,
        out_specs=(
            P(("dp", "cp"), None),
            P(("dp", "cp"), None),
            P(("dp", "cp"), None),
            P(),
            P(),
            P(),
        ),
        check_vma=False,
    )
```

profile of v0, /device:TPU:1, one launch (start us, length us, event | category | flops | bytes accessed | tf_op | source)
XLA Modules:
  0.0 425.6 jit_solution(10073714078295284084)
XLA Ops:
  10.1 20.9 %all_to_all.27 = s32[128,1,4]{2,1,0:T(1,128)S(1)} all-to-all(s32[128,1,4]{2,1,0:T(1,128)S(1)} %bitcast.196), channel_id=1, replica_groups=mesh['dp'=8,'cp'=16] {'dp','cp'}, dimensions={0} | all-to-all | bytes 4096 | tf_op jit(solution)/shard_map/all_to_all | solution.py:128
  31.7 3.1 gather_fusion
  39.7 4.5 %all-to-all-start.1 = ((bf16[128,4,512]{2,1,0:T(4,128)(2,1)}), bf16[128,4,512]{2,1,0:T(4,128)(2,1)S(1)}, u32[]{:S(2)}, u32[]{:S(2)}) async-start(bf16[128,4,512]{2,1,0:T(4,128)(2,1)} %pad_select_fusion), calls=%async_computation.1 | async-start | bytes 1048576 | tf_op jit(solution)/shard_map/all_to_all | solution.py:142
  44.9 12.7 %all-to-all-done.1 = bf16[128,4,512]{2,1,0:T(4,128)(2,1)S(1)} async-done(((bf16[128,4,512]{2,1,0:T(4,128)(2,1)}), bf16[128,4,512]{2,1,0:T(4,128)(2,1)S(1)}, u32[]{:S(2)}, u32[]{:S(2)}) %all-to-all-start.1) | async-done | bytes 524320 | tf_op jit(solution)/shard_map/all_to_all | solution.py:142
  63.7 45.9 %all-gather.3.cloned.1.call-done = bf16[2048,1024]{1,0:T(8,128)(2,1)} async-done(((bf16[128,1024]{1,0:T(8,128)(2,1)}), bf16[2048,1024]{1,0:T(8,128)(2,1)}) %all-gather.3.cloned.1.call-update) | async-done | bytes 4194320 | tf_op jit(solution)/shard_map/all_gather | solution.py:18
  109.6 4.5 %fusion.84 = (bf16[2048,512]{1,0:T(8,128)(2,1)}, bf16[2048,512]{1,0:T(8,128)(2,1)}) fusion(bf16[2048,1024]{1,0:T(8,128)(2,1)} %all-gather.3.cloned.1.call-done), kind=kLoop, calls=%fused_computation.161 | loop fusion | bytes 8388608 | tf_op jit(solution)/shard_map/split | solution.py:18
  114.2 4.0 copy.83
  118.1 4.0 copy.84
  122.8 6.8 %while.38 = (s32[]{:T(128)}, f32[128,8,64]{0,2,1:T(8,128)}, s32[]{:T(128)}, bf16[2048,512]{0,1:T(8,128)(2,1)}, bf16[2048,512]{0,1:T(8,128)(2,1)}, /*index=5*/bf1...) while((s32[]{:T(128)}, f32[128,8,64]{0,2,1:T(8,128)}, ...), condition=%wide.region_5.6_spmd.clone, body=%wide.region_4.5_spmd.clone.sunk | while | flops 275973248 | bytes 7218343 | solution.py:196
  125.7 3.9 fusion.132
  139.3 11.6 %while.40 = (s32[]{:T(128)}, f32[128,8,64]{0,2,1:T(8,128)}, s32[]{:T(128)}, bf16[2048,512]{0,1:T(8,128)(2,1)}, bf16[2048,512]{0,1:T(8,128)(2,1)}, /*index=5*/bf1...) while((s32[]{:T(128)}, f32[128,8,64]{0,2,1:T(8,128)}, ...), condition=%wide.region_17.18_spmd.clone, body=%wide.region_16.17_spmd.clone.sunk | while | flops 415433856 | bytes 16786608 | solution.py:236
  145.0 5.8 %fusion.139 = f32[128,8,64]{0,2,1:T(8,128)} fusion(f32[128,8,64]{0,2,1:T(8,128)} %get-tuple-element.860, bf16[1024,8,64]{0,2,1:T(8,128)(2,1)S(1)} %bitcast.180, f32[8,1024,128]{2,1,0:T(8,128)} %fusion.138, bf16[1024,8,64]{0,2,1:T(8,128)(2,1)} %bitcast.183, bf16[128,8,64]{0,2,1:T(8,128)(2,1)} %get-tuple-element.876, ...), kind=kOutput, calls=%fused_computation.62.clone.1 | convolution fusion | flops 281083904 | bytes 7077888 | tf_op jit(solution)/shard_map/while/body/hqk,khd->qhd/dot_general | solution.py:231
  154.7 41.7 %all-gather.5.cloned.1.call-done = bf16[2048,1024]{1,0:T(8,128)(2,1)} async-done(((bf16[128,1024]{1,0:T(8,128)(2,1)}), bf16[2048,1024]{1,0:T(8,128)(2,1)}) %all-gather.5.cloned.1.call-update) | async-done | bytes 4194320 | tf_op jit(solution)/shard_map/all_gather | solution.py:18
  196.4 4.5 %fusion.83 = (bf16[2048,512]{1,0:T(8,128)(2,1)}, bf16[2048,512]{1,0:T(8,128)(2,1)}) fusion(bf16[2048,1024]{1,0:T(8,128)(2,1)} %all-gather.5.cloned.1.call-done), kind=kLoop, calls=%fused_computation.160 | loop fusion | bytes 8388608 | tf_op jit(solution)/shard_map/split | solution.py:18
  200.9 4.0 copy.88
  204.9 4.0 copy.89
  209.6 39.0 %while.39 = (s32[]{:T(128)}, f32[128,8,64]{0,2,1:T(8,128)S(1)}, f32[128,8,64]{0,2,1:T(8,128)}, s32[]{:T(128)}, bf16[2048,512]{0,1:T(8,128)(2,1)}, /*index=5*/bf1...) while((s32[]{:T(128)}, f32[128,8,64]{0,2,1:T(8,128)S(1)}, ...), condition=%wide.region_15.16_spmd.clone, body=%wide.region_11.15_spmd.clone.sunk | while | flops 557058176 | bytes 24783208 | solution.py:276
  211.5 17.6 %conditional.3 = ((f32[128,8,64]{0,2,1:T(8,128)S(1)}, f32[128,8,64]{0,2,1:T(8,128)})) conditional(s32[]{:T(128)} %convert_element_type.220, (f32[128,8,64]{0,2,1:T(8,128)S(1)}, f32[128,8,64]{0,2,1:T(8,128)}) %tuple.126, (s32[]{:T(128)}, s32[1024]{0:T(1024)S(1)}, s32[]{:T(128)}, bf16[2048,512]{0,1:T(8,128)(2,1)}, bf16[128,8,64]{0,2,1:T(8,128)(2,1)}, ...), branch_computations={%region_13.13_spmd, %region_14.14_spmd} | conditional | flops 557056128 | bytes 24778362 | solution.py:272
  218.6 5.9 %fusion.11 = f32[128,8,64]{0,2,1:T(8,128)} fusion(f32[128,8,64]{0,2,1:T(8,128)} %copy-done.8, bf16[1024,8,64]{0,2,1:T(8,128)(2,1)S(1)} %bitcast.182, f32[8,1024,128]{2,1,0:T(8,128)} %fusion.88, bf16[1024,8,64]{0,2,1:T(8,128)(2,1)} %bitcast.186, bf16[128,8,64]{0,2,1:T(8,128)(2,1)} %get-tuple-element.319, pred[1024,128]{1,0:T(8,128)(4,1)} %broadcast_compare_fusion), kind=kOutput, calls=%fused_computation.18 | convolution fusion | flops 281083904 | bytes 7077888 | tf_op jit(solution)/shard_map/while/body/eval_jaxpr/cond/branch_1_fun/hqk,qhd->khd/dot_general | solution.py:264
  224.4 4.7 %fusion.10 = f32[128,8,64]{0,2,1:T(8,128)} fusion(f32[128,8,64]{0,2,1:T(8,128)} %get-tuple-element.322, bf16[1024,8,64]{0,2,1:T(8,128)(2,1)} %bitcast.187, f32[8,1024,128]{2,1,0:T(8,128)} %fusion.88, pred[1024,128]{1,0:T(8,128)(4,1)} %broadcast_compare_fusion), kind=kOutput, calls=%fused_computation.17 | convolution fusion | flops 141623296 | bytes 5898240 | tf_op jit(solution)/shard_map/while/body/eval_jaxpr/cond/branch_1_fun/hqk,qhd->khd/dot_general | solution.py:267
  231.0 17.6 %conditional.3 = ((f32[128,8,64]{0,2,1:T(8,128)S(1)}, f32[128,8,64]{0,2,1:T(8,128)})) conditional(s32[]{:T(128)} %convert_element_type.220, (f32[128,8,64]{0,2,1:T(8,128)S(1)}, f32[128,8,64]{0,2,1:T(8,128)}) %tuple.126, (s32[]{:T(128)}, s32[1024]{0:T(1024)S(1)}, s32[]{:T(128)}, bf16[2048,512]{0,1:T(8,128)(2,1)}, bf16[128,8,64]{0,2,1:T(8,128)(2,1)}, ...), branch_computations={%region_13.13_spmd, %region_14.14_spmd} | conditional | flops 557056128 | bytes 24778362 | solution.py:272
  234.4 2.8 fusion.88
  238.1 5.9 %fusion.11 = f32[128,8,64]{0,2,1:T(8,128)} fusion(f32[128,8,64]{0,2,1:T(8,128)} %copy-done.8, bf16[1024,8,64]{0,2,1:T(8,128)(2,1)S(1)} %bitcast.182, f32[8,1024,128]{2,1,0:T(8,128)} %fusion.88, bf16[1024,8,64]{0,2,1:T(8,128)(2,1)} %bitcast.186, bf16[128,8,64]{0,2,1:T(8,128)(2,1)} %get-tuple-element.319, pred[1024,128]{1,0:T(8,128)(4,1)} %broadcast_compare_fusion), kind=kOutput, calls=%fused_computation.18 | convolution fusion | flops 281083904 | bytes 7077888 | tf_op jit(solution)/shard_map/while/body/eval_jaxpr/cond/branch_1_fun/hqk,qhd->khd/dot_general | solution.py:264
  243.9 4.7 %fusion.10 = f32[128,8,64]{0,2,1:T(8,128)} fusion(f32[128,8,64]{0,2,1:T(8,128)} %get-tuple-element.322, bf16[1024,8,64]{0,2,1:T(8,128)(2,1)} %bitcast.187, f32[8,1024,128]{2,1,0:T(8,128)} %fusion.88, pred[1024,128]{1,0:T(8,128)(4,1)} %broadcast_compare_fusion), kind=kOutput, calls=%fused_computation.17 | convolution fusion | flops 141623296 | bytes 5898240 | tf_op jit(solution)/shard_map/while/body/eval_jaxpr/cond/branch_1_fun/hqk,qhd->khd/dot_general | solution.py:267
  264.5 7.3 %all-to-all-start.2 = ((bf16[128,1,2,512]{3,2,1,0:T(2,128)(2,1)}), bf16[128,1,2,512]{3,2,1,0:T(2,128)(2,1)S(1)}, u32[]{:S(2)}, u32[]{:S(2)}) async-start(bf16[128,1,2,512]{3,2,1,0:T(2,128)(2,1)} %get-tuple-element.591), calls=%async_computation.2 | async-start | bytes 524288 | tf_op jit(solution)/shard_map/all_to_all | solution.py:44
  274.0 9.4 %all-to-all-done.2 = bf16[128,1,2,512]{3,2,1,0:T(2,128)(2,1)S(1)} async-done(((bf16[128,1,2,512]{3,2,1,0:T(2,128)(2,1)}), bf16[128,1,2,512]{3,2,1,0:T(2,128)(2,1)S(1)}, u32[]{:S(2)}, u32[]{:S(2)}) %all-to-all-start.2) | async-done | bytes 262176 | tf_op jit(solution)/shard_map/all_to_all | solution.py:44
  283.5 5.3 %all-to-all-start.3 = ((bf16[128,1,2,512]{3,2,1,0:T(2,128)(2,1)}), bf16[128,1,2,512]{3,2,1,0:T(2,128)(2,1)}, u32[]{:S(2)}, u32[]{:S(2)}) async-start(bf16[128,1,2,512]{3,2,1,0:T(2,128)(2,1)} %get-tuple-element.592), calls=%async_computation.3 | async-start | bytes 524288 | tf_op jit(solution)/shard_map/all_to_all | solution.py:44
  290.8 8.9 %all-to-all-done.3 = bf16[128,1,2,512]{3,2,1,0:T(2,128)(2,1)} async-done(((bf16[128,1,2,512]{3,2,1,0:T(2,128)(2,1)}), bf16[128,1,2,512]{3,2,1,0:T(2,128)(2,1)}, u32[]{:S(2)}, u32[]{:S(2)}) %all-to-all-start.3) | async-done | bytes 262176 | tf_op jit(solution)/shard_map/all_to_all | solution.py:44
  304.4 5.2 %scatter_custom_fusion.2 = f32[512,512]{1,0:T(8,128)} fusion(s32[512]{0:T(512)S(1)} %bitcast.200, f32[512,512]{1,0:T(8,128)} %reshape.449, f32[]{:T(128)} %constant.155.clone.1), kind=kCustom, calls=%fused_computation.89 | custom fusion | flops 262144 | bytes 1049088 | tf_op jit(solution)/shard_map/scatter-add | solution.py:323
  309.6 3.2 scatter_custom_fusion.3
  312.9 100.2 %all-reduce.5.cloned.1.call-done = (bf16[128,512]{1,0:T(8,128)(2,1)}, bf16[512,2048]{1,0:T(8,128)(2,1)}, bf16[512,512]{1,0:T(8,128)(2,1)}) async-done(((bf16[128,512]{1,0:T(8,128)(2,1)}, bf16[512,2048]{1,0:T(8,128)(2,1)}, bf16[512,512]{1,0:T(8,128)(2,1)}), (bf16[128,512]{1,0:T(8,128)(2,1)}, bf16[512,2048]{1,0:T(8,128)(2,1)}, bf16[512,512]{1,0:T(8,128)(2,1)})) %all-reduce.5.cloned.1.call-update) | async-done | bytes 2752528 | tf_op jit(solution)/shard_map/psum | solution.py:295
  413.0 4.2 convert_multiply_fusion
  (160 shorter events, 77.7 us)
Async XLA Ops:
  7.2 52.4 %copy-start = (bf16[512,2048]{1,0:T(8,128)(2,1)S(1)}, bf16[512,2048]{1,0:T(8,128)(2,1)}, u32[]{:S(2)}) copy-start(bf16[512,2048]{1,0:T(8,128)(2,1)} %param.21) | copy-start | bytes 6291460
  7.2 28.7 %copy-start.4 = (bf16[2048,128]{1,0:T(8,128)(2,1)S(1)}, bf16[2048,128]{1,0:T(8,128)(2,1)}, u32[]{:S(2)}) copy-start(bf16[2048,128]{1,0:T(8,128)(2,1)} %param.19) | copy-start | bytes 1572868
  8.9 35.4 %copy-start.26 = (s32[128]{0:T(128)}, s32[128]{0:T(128)S(1)}, u32[]{:S(2)}) copy-start(s32[128]{0:T(128)S(1)} %fusion.76) | copy-start | bytes 1540
  31.7 12.6 %copy-start.27 = (s32[128]{0:T(128)S(1)}, s32[128]{0:T(128)}, u32[]{:S(2)}) copy-start(s32[128]{0:T(128)} %param.17) | copy-start | bytes 1540
  34.8 23.7 %copy-start.15 = (bf16[128,512]{1,0:T(8,128)(2,1)S(1)}, bf16[128,512]{1,0:T(8,128)(2,1)}, u32[]{:S(2)}) copy-start(bf16[128,512]{1,0:T(8,128)(2,1)} %param.20) | copy-start | bytes 393220
  39.7 17.9 %all-to-all-start.1 = ((bf16[128,4,512]{2,1,0:T(4,128)(2,1)}), bf16[128,4,512]{2,1,0:T(4,128)(2,1)S(1)}, u32[]{:S(2)}, u32[]{:S(2)}) async-start(bf16[128,4,512]{2,1,0:T(4,128)(2,1)} %pad_select_fusion), calls=%async_computation.1 | async-start | bytes 1048576 | tf_op jit(solution)/shard_map/all_to_all | solution.py:142
  44.2 65.4 %all-gather.3.cloned.1.call-start = ((), (), s32[]{:S(2)}) async-start(), calls=%async_computation.4 | async-start | bytes 4456448 | tf_op jit(solution)/shard_map/all_gather | solution.py:18
  44.9 16.2 %copy-start.23 = (pred[128]{0:T(512)(128)(4,1)}, pred[128]{0:T(512)(128)(4,1)S(1)}, u32[]{:S(2)}) copy-start(pred[128]{0:T(512)(128)(4,1)S(1)} %get-tuple-element.603) | copy-start | bytes 388
  58.8 0.7 copy-start.1
  58.8 2.2 copy-start.19
  59.5 1.5 copy-start.21
  61.0 53.1 %copy-start.12 = (bf16[128,2048]{1,0:T(8,128)(2,1)}, bf16[128,2048]{1,0:T(8,128)(2,1)S(1)}, u32[]{:S(2)}) copy-start(bf16[128,2048]{1,0:T(8,128)(2,1)S(1)} %get-tuple-element.606) | copy-start | bytes 1572868
  61.1 53.1 %copy-start.6 = (bf16[128,512]{1,0:T(8,128)(2,1)}, bf16[128,512]{1,0:T(8,128)(2,1)S(1)}, u32[]{:S(2)}) copy-start(bf16[128,512]{1,0:T(8,128)(2,1)S(1)} %get-tuple-element.593) | copy-start | bytes 393220
  62.0 134.4 %all-gather.5.cloned.1.call-start = ((), (), s32[]{:S(2)}) async-start(), calls=%async_computation.5 | async-start | bytes 4456448 | tf_op jit(solution)/shard_map/all_gather | solution.py:18
  138.5 274.5 %all-reduce.5.cloned.1.call-start = ((), (), s32[]{:S(2)}) async-start(), calls=%async_computation.6 | async-start | bytes 5505024 | tf_op jit(solution)/shard_map/psum | solution.py:295
  209.6 43.7 %copy-start.2 = (f32[128,512]{1,0:T(8,128)S(1)}, f32[128,512]{1,0:T(8,128)}, u32[]{:S(2)}) copy-start(f32[128,512]{1,0:T(8,128)} %copy-done.1) | copy-start | bytes 786436
  209.6 43.7 %copy-start.20 = (f32[128]{0:T(128)S(1)}, f32[128]{0:T(128)}, u32[]{:S(2)}) copy-start(f32[128]{0:T(128)} %copy-done.19) | copy-start | bytes 1540
  209.6 43.7 %copy-start.22 = (f32[128]{0:T(128)S(1)}, f32[128]{0:T(128)}, u32[]{:S(2)}) copy-start(f32[128]{0:T(128)} %copy-done.21) | copy-start | bytes 1540
  211.5 0.7 copy-start.8
  224.4 4.7 %copy-start.9 = (f32[128,8,64]{0,2,1:T(8,128)S(1)}, f32[128,8,64]{0,2,1:T(8,128)}, u32[]{:S(2)}) copy-start(f32[128,8,64]{0,2,1:T(8,128)} %fusion.11) | copy-start | bytes 786436 | tf_op jit(solution)/shard_map/while/body/eval_jaxpr/cond
  243.9 4.7 %copy-start.9 = (f32[128,8,64]{0,2,1:T(8,128)S(1)}, f32[128,8,64]{0,2,1:T(8,128)}, u32[]{:S(2)}) copy-start(f32[128,8,64]{0,2,1:T(8,128)} %fusion.11) | copy-start | bytes 786436 | tf_op jit(solution)/shard_map/while/body/eval_jaxpr/cond
  251.5 4.9 %copy-start.5 = (bf16[128,512]{1,0:T(8,128)(2,1)S(1)}, bf16[128,512]{1,0:T(8,128)(2,1)}, u32[]{:S(2)}) copy-start(bf16[128,512]{1,0:T(8,128)(2,1)} %param.23) | copy-start | bytes 393220
  251.5 5.1 %copy-start.25 = (pred[128]{0:T(512)(128)(4,1)S(1)}, pred[128]{0:T(512)(128)(4,1)}, u32[]{:S(2)}) copy-start(pred[128]{0:T(512)(128)(4,1)} %get-tuple-element.602) | copy-start | bytes 388
  255.5 3.1 copy-start.16
  255.5 4.0 copy-start.24
  256.6 2.0 copy-start.3
  258.5 30.3 %copy-start.7 = (bf16[128,512]{1,0:T(8,128)(2,1)S(1)}, bf16[128,512]{1,0:T(8,128)(2,1)}, u32[]{:S(2)}) copy-start(bf16[128,512]{1,0:T(8,128)(2,1)} %get-tuple-element.587) | copy-start | bytes 393220
  264.5 19.0 %all-to-all-start.2 = ((bf16[128,1,2,512]{3,2,1,0:T(2,128)(2,1)}), bf16[128,1,2,512]{3,2,1,0:T(2,128)(2,1)S(1)}, u32[]{:S(2)}, u32[]{:S(2)}) async-start(bf16[128,1,2,512]{3,2,1,0:T(2,128)(2,1)} %get-tuple-element.591), calls=%async_computation.2 | async-start | bytes 524288 | tf_op jit(solution)/shard_map/all_to_all | solution.py:44
  283.5 7.3 %copy-start.11 = (bf16[128,1,2,512]{3,2,1,0:T(2,128)(2,1)}, bf16[128,1,2,512]{3,2,1,0:T(2,128)(2,1)S(1)}, u32[]{:S(2)}) copy-start(bf16[128,1,2,512]{3,2,1,0:T(2,128)(2,1)S(1)} %all-to-all-done.2) | copy-start | bytes 786436
  283.5 16.2 %all-to-all-start.3 = ((bf16[128,1,2,512]{3,2,1,0:T(2,128)(2,1)}), bf16[128,1,2,512]{3,2,1,0:T(2,128)(2,1)}, u32[]{:S(2)}, u32[]{:S(2)}) async-start(bf16[128,1,2,512]{3,2,1,0:T(2,128)(2,1)} %get-tuple-element.592), calls=%async_computation.3 | async-start | bytes 524288 | tf_op jit(solution)/shard_map/all_to_all | solution.py:44
  413.0 4.2 copy-start.14
  413.0 5.3 %copy-start.18 = (bf16[128,512]{1,0:T(8,128)(2,1)S(1)}, bf16[128,512]{1,0:T(8,128)(2,1)}, u32[]{:S(2)}) copy-start(bf16[128,512]{1,0:T(8,128)(2,1)} %get-tuple-element.571) | copy-start | bytes 393220
  (4 other events, 2.8 us)
Sparse Core Ops, SparseCore 0:
  62.1 47.4 all-gather.2
  138.6 57.7 all-gather.4
  258.7 154.2 all-reduce.4
where the time goes:
time: 427 us; the launch traced here: 426 us
  waiting for transfers between devices  219 us (51%)
  local copies, waits for them, and re-layouts  60.9 us (14%)
  matrix products  53.4 us (13%)
  other arithmetic  37.6 us (9%)
  blocking collectives  20.9 us (5%)
  starting transfers between devices  17.2 us (4%)
  between operations  14.2 us (3%)
    psum x1, waiting for transfers between devices, local(): lax.psum(projection_local.astype(jnp.bfloat16), ('dp', 'cp'))  100 us
    all_gather x2, waiting for transfers between devices, side_by_side(): lax.all_gather(both, axis, axis=dim, tiled=True)  87.6 us
    all_to_all x1, blocking collectives, local(): lax.all_to_all(requests, ('dp', 'cp'), split_axis=0, concat_axis=0, tiled...  20.9 us
    all_to_all x2, waiting for transfers between devices, several_exchanges(): lax.all_to_all(piece, axis, split_axis=0, concat_axis=0, tiled=True)  18.4 us
    unnamed x56, local copies, waits for them, and re-layouts  17.1 us
    all_to_all x1, waiting for transfers between devices, local(): lax.all_to_all(packed, ('dp', 'cp'), split_axis=0, concat_axis=0, tiled=T...  12.7 us
    all_to_all x2, starting transfers between devices, several_exchanges(): lax.all_to_all(piece, axis, split_axis=0, concat_axis=0, tiled=True)  12.6 us
    dot_general x2, matrix products, accumulate(): jnp.einsum('hqk,qhd->khd', delta_scores, query_block, preferred_element_t...  11.7 us
  transfers between devices with their start and end apart: 6, of which 6 were waited for; matrix products, arithmetic and copies ran while one was open for 10% of the time, Pallas kernels for 0%

commit v1 on v0

--- a/solution.py
+++ b/solution.py
@@ -7,6 +7,11 @@
 HEADS = 8
 EPSILON = 1e-05
 block_limit = 1024
+
+
+def by_each_axis(array, leading, second):
+    half = lax.psum(array, leading)
+    return lax.psum(half, second)
 
 
 def side_by_side(arrays, axis, dim, along):
@@ -292,7 +297,7 @@
     joined_sum, output_sum, projection_sum = (
         lax.psum(joined_local.astype(jnp.bfloat16), ("dp", "cp")).astype(jnp.float32),
         lax.psum(output_local.astype(jnp.bfloat16), ("dp", "cp")).astype(jnp.float32),
-        lax.psum(projection_local.astype(jnp.bfloat16), ("dp", "cp")).astype(jnp.float32),
+        by_each_axis(projection_local.astype(jnp.bfloat16), "cp", "dp").astype(jnp.float32),
     )
     norm_scale = (tokens_here * devices) ** (-0.5)
     cold_event = jnp.where(

time: 427 us -> 571 us (1.34)
  waiting for transfers between devices: 219 us -> 361 us
    psum x1 -> x3, waiting for transfers between devices: 100 us -> 250 us  [the longest x1 144 us: local(): lax.psum(joined_local.astype(jnp.bfloat16), ('dp', 'cp'))]
    all_to_all x2, waiting for transfers between devices: 18.4 us -> 8.85 us  [several_exchanges(): lax.all_to_all(piece, axis, split_axis=0, concat_axis=0, tiled=True)]
    unnamed x56 -> x52, local copies, waits for them, and re-layouts: 17.1 us -> 16.4 us
  transfers between devices with their start and end apart: 6 -> 8, of which waited for: 6 -> 7; matrix products, arithmetic and copies ran while one was open for 10% -> 8% of each run, Pallas kernels for 0% -> 0%
where the time goes in v1:
time: 571 us; the launch traced here: 570 us
  waiting for transfers between devices  361 us (63%)
  local copies, waits for them, and re-layouts  60 us (11%)
  matrix products  52.6 us (9%)
  other arithmetic  38.4 us (7%)
  blocking collectives  20.9 us (4%)
  starting transfers between devices  19.7 us (3%)
  between operations  14.3 us (3%)
    psum x1, waiting for transfers between devices, local(): lax.psum(joined_local.astype(jnp.bfloat16), ('dp', 'cp'))  144 us
    all_gather x2, waiting for transfers between devices, side_by_side(): lax.all_gather(both, axis, axis=dim, tiled=True)  89.7 us
    psum x1, waiting for transfers between devices, by_each_axis(): half = lax.psum(array, leading)  78.9 us
    psum x1, waiting for transfers between devices, by_each_axis(): return lax.psum(half, second)  26.5 us
    all_to_all x1, blocking collectives, local(): lax.all_to_all(requests, ('dp', 'cp'), split_axis=0, concat_axis=0, tiled...  20.9 us
    unnamed x52, local copies, waits for them, and re-layouts  16.4 us
    all_to_all x2, starting transfers between devices, several_exchanges(): lax.all_to_all(piece, axis, split_axis=0, concat_axis=0, tiled=True)  14.8 us
    all_to_all x1, waiting for transfers between devices, local(): lax.all_to_all(packed, ('dp', 'cp'), split_axis=0, concat_axis=0, tiled=T...  12.8 us
  transfers between devices with their start and end apart: 8, of which 7 were waited for; matrix products, arithmetic and copies ran while one was open for 8% of the time, Pallas kernels for 0%

profile of v1, /device:TPU:1, one launch (start us, length us, event | category | flops | bytes accessed | tf_op | source)
XLA Modules:
  0.0 569.5 jit_solution(1757749743465349953)
XLA Ops:
  10.1 20.9 %all_to_all.27 = s32[128,1,4]{2,1,0:T(1,128)S(1)} all-to-all(s32[128,1,4]{2,1,0:T(1,128)S(1)} %bitcast.196), channel_id=1, replica_groups=mesh['dp'=8,'cp'=16] {'dp','cp'}, dimensions={0} | all-to-all | bytes 4096 | tf_op jit(solution)/shard_map/all_to_all | solution.py:133
  31.7 3.1 gather_fusion
  39.7 4.5 all-to-all-start.1
  44.8 12.8 %all-to-all-done.1 = bf16[128,4,512]{2,1,0:T(4,128)(2,1)S(1)} async-done(((bf16[128,4,512]{2,1,0:T(4,128)(2,1)}), bf16[128,4,512]{2,1,0:T(4,128)(2,1)S(1)}, u32[]{:S(2)}, u32[]{:S(2)}) %all-to-all-start.1) | async-done | bytes 524320 | tf_op jit(solution)/shard_map/all_to_all | solution.py:147
  63.7 45.9 %all-gather.3.cloned.1.call-done = bf16[2048,1024]{1,0:T(8,128)(2,1)} async-done(((bf16[128,1024]{1,0:T(8,128)(2,1)}), bf16[2048,1024]{1,0:T(8,128)(2,1)}) %all-gather.3.cloned.1.call-update) | async-done | bytes 4194320 | tf_op jit(solution)/shard_map/all_gather | solution.py:23
  109.6 4.5 fusion.84
  114.1 4.0 copy.83
  118.1 4.0 copy.84
  122.7 6.8 %while.38 = (s32[]{:T(128)}, f32[128,8,64]{0,2,1:T(8,128)}, s32[]{:T(128)}, bf16[2048,512]{0,1:T(8,128)(2,1)}, bf16[2048,512]{0,1:T(8,128)(2,1)}, /*index=5*/bf1...) while((s32[]{:T(128)}, f32[128,8,64]{0,2,1:T(8,128)}, ...), condition=%wide.region_5.6_spmd.clone, body=%wide.region_4.5_spmd.clone.sunk | while | flops 275973248 | bytes 7218343 | solution.py:201
  125.6 3.9 fusion.132
  139.2 11.6 %while.40 = (s32[]{:T(128)}, f32[128,8,64]{0,2,1:T(8,128)}, s32[]{:T(128)}, bf16[2048,512]{0,1:T(8,128)(2,1)}, bf16[2048,512]{0,1:T(8,128)(2,1)}, /*index=5*/bf1...) while((s32[]{:T(128)}, f32[128,8,64]{0,2,1:T(8,128)}, ...), condition=%wide.region_17.18_spmd.clone, body=%wide.region_16.17_spmd.clone.sunk | while | flops 415433856 | bytes 16786608 | solution.py:241
  145.0 5.8 %fusion.139 = f32[128,8,64]{0,2,1:T(8,128)} fusion(f32[128,8,64]{0,2,1:T(8,128)} %get-tuple-element.859, bf16[1024,8,64]{0,2,1:T(8,128)(2,1)S(1)} %bitcast.180, f32[8,1024,128]{2,1,0:T(8,128)} %fusion.138, bf16[1024,8,64]{0,2,1:T(8,128)(2,1)} %bitcast.183, bf16[128,8,64]{0,2,1:T(8,128)(2,1)} %get-tuple-element.875, ...), kind=kOutput, calls=%fused_computation.62.clone.1 | convolution fusion | flops 281083904 | bytes 7077888 | tf_op jit(solution)/shard_map/while/body/hqk,khd->qhd/dot_general | solution.py:236
  152.6 43.8 %all-gather.5.cloned.1.call-done = bf16[2048,1024]{1,0:T(8,128)(2,1)} async-done(((bf16[128,1024]{1,0:T(8,128)(2,1)}), bf16[2048,1024]{1,0:T(8,128)(2,1)}) %all-gather.5.cloned.1.call-update) | async-done | bytes 4194320 | tf_op jit(solution)/shard_map/all_gather | solution.py:23
  196.4 4.5 fusion.83
  200.9 4.0 copy.88
  204.9 4.0 copy.89
  209.6 39.1 %while.39 = (s32[]{:T(128)}, f32[128,8,64]{0,2,1:T(8,128)S(1)}, f32[128,8,64]{0,2,1:T(8,128)}, s32[]{:T(128)}, bf16[2048,512]{0,1:T(8,128)(2,1)}, /*index=5*/bf1...) while((s32[]{:T(128)}, f32[128,8,64]{0,2,1:T(8,128)S(1)}, ...), condition=%wide.region_15.16_spmd.clone, body=%wide.region_11.15_spmd.clone.sunk | while | flops 557058176 | bytes 24783208 | solution.py:281
  211.5 17.7 %conditional.3 = ((f32[128,8,64]{0,2,1:T(8,128)S(1)}, f32[128,8,64]{0,2,1:T(8,128)})) conditional(s32[]{:T(128)} %convert_element_type.220, (f32[128,8,64]{0,2,1:T(8,128)S(1)}, f32[128,8,64]{0,2,1:T(8,128)}) %tuple.126, (s32[]{:T(128)}, s32[1024]{0:T(1024)S(1)}, s32[]{:T(128)}, bf16[2048,512]{0,1:T(8,128)(2,1)}, bf16[128,8,64]{0,2,1:T(8,128)(2,1)}, ...), branch_computations={%region_13.13_spmd, %region_14.14_spmd} | conditional | flops 557056128 | bytes 24778362 | solution.py:277
  218.6 5.9 %fusion.11 = f32[128,8,64]{0,2,1:T(8,128)} fusion(f32[128,8,64]{0,2,1:T(8,128)} %copy-done.8, bf16[1024,8,64]{0,2,1:T(8,128)(2,1)S(1)} %bitcast.182, f32[8,1024,128]{2,1,0:T(8,128)} %fusion.88, bf16[1024,8,64]{0,2,1:T(8,128)(2,1)} %bitcast.186, bf16[128,8,64]{0,2,1:T(8,128)(2,1)} %get-tuple-element.319, pred[1024,128]{1,0:T(8,128)(4,1)} %broadcast_compare_fusion), kind=kOutput, calls=%fused_computation.18 | convolution fusion | flops 281083904 | bytes 7077888 | tf_op jit(solution)/shard_map/while/body/eval_jaxpr/cond/branch_1_fun/hqk,qhd->khd/dot_general | solution.py:269
  224.5 4.7 fusion.10
  231.1 17.7 %conditional.3 = ((f32[128,8,64]{0,2,1:T(8,128)S(1)}, f32[128,8,64]{0,2,1:T(8,128)})) conditional(s32[]{:T(128)} %convert_element_type.220, (f32[128,8,64]{0,2,1:T(8,128)S(1)}, f32[128,8,64]{0,2,1:T(8,128)}) %tuple.126, (s32[]{:T(128)}, s32[1024]{0:T(1024)S(1)}, s32[]{:T(128)}, bf16[2048,512]{0,1:T(8,128)(2,1)}, bf16[128,8,64]{0,2,1:T(8,128)(2,1)}, ...), branch_computations={%region_13.13_spmd, %region_14.14_spmd} | conditional | flops 557056128 | bytes 24778362 | solution.py:277
  238.2 5.9 %fusion.11 = f32[128,8,64]{0,2,1:T(8,128)} fusion(f32[128,8,64]{0,2,1:T(8,128)} %copy-done.8, bf16[1024,8,64]{0,2,1:T(8,128)(2,1)S(1)} %bitcast.182, f32[8,1024,128]{2,1,0:T(8,128)} %fusion.88, bf16[1024,8,64]{0,2,1:T(8,128)(2,1)} %bitcast.186, bf16[128,8,64]{0,2,1:T(8,128)(2,1)} %get-tuple-element.319, pred[1024,128]{1,0:T(8,128)(4,1)} %broadcast_compare_fusion), kind=kOutput, calls=%fused_computation.18 | convolution fusion | flops 281083904 | bytes 7077888 | tf_op jit(solution)/shard_map/while/body/eval_jaxpr/cond/branch_1_fun/hqk,qhd->khd/dot_general | solution.py:269
  244.1 4.7 fusion.10
  256.9 78.9 %all-reduce.7.cloned.1.call-done = bf16[128,512]{1,0:T(8,128)(2,1)} async-done(((bf16[128,512]{1,0:T(8,128)(2,1)}), bf16[128,512]{1,0:T(8,128)(2,1)}) %all-reduce.7.cloned.1.call-update) | async-done | bytes 131088 | tf_op jit(solution)/shard_map/psum | solution.py:13
  344.2 9.6 %all-to-all-start.2 = ((bf16[128,1,2,512]{3,2,1,0:T(2,128)(2,1)}), bf16[128,1,2,512]{3,2,1,0:T(2,128)(2,1)S(1)}, u32[]{:S(2)}, u32[]{:S(2)}) async-start(bf16[128,1,2,512]{3,2,1,0:T(2,128)(2,1)} %get-tuple-element.590), calls=%async_computation.2 | async-start | bytes 524288 | tf_op jit(solution)/shard_map/all_to_all | solution.py:49
  356.0 8.8 %all-to-all-done.2 = bf16[128,1,2,512]{3,2,1,0:T(2,128)(2,1)S(1)} async-done(((bf16[128,1,2,512]{3,2,1,0:T(2,128)(2,1)}), bf16[128,1,2,512]{3,2,1,0:T(2,128)(2,1)S(1)}, u32[]{:S(2)}, u32[]{:S(2)}) %all-to-all-start.2) | async-done | bytes 262176 | tf_op jit(solution)/shard_map/all_to_all | solution.py:49
  364.9 5.2 all-to-all-start.3
  372.1 26.5 %all-reduce.9.cloned.1.call-done = bf16[128,512]{1,0:T(8,128)(2,1)} async-done(((bf16[128,512]{1,0:T(8,128)(2,1)}), bf16[128,512]{1,0:T(8,128)(2,1)}) %all-reduce.9.cloned.1.call-update) | async-done | bytes 131088 | tf_op jit(solution)/shard_map/psum | solution.py:14
  404.9 5.2 scatter_custom_fusion.2
  410.1 3.2 scatter_custom_fusion.3
  413.4 144.3 %all-reduce.11.cloned.1.call-done = (bf16[512,2048]{1,0:T(8,128)(2,1)}, bf16[512,512]{1,0:T(8,128)(2,1)}) async-done(((bf16[512,2048]{1,0:T(8,128)(2,1)}, bf16[512,512]{1,0:T(8,128)(2,1)}), (bf16[512,2048]{1,0:T(8,128)(2,1)}, bf16[512,512]{1,0:T(8,128)(2,1)})) %all-reduce.11.cloned.1.call-update) | async-done | bytes 2621456 | tf_op jit(solution)/shard_map/psum | solution.py:298
  557.7 4.2 convert_multiply_fusion
  (162 shorter events, 79.9 us)
Async XLA Ops:
  7.2 52.4 %copy-start = (bf16[512,2048]{1,0:T(8,128)(2,1)S(1)}, bf16[512,2048]{1,0:T(8,128)(2,1)}, u32[]{:S(2)}) copy-start(bf16[512,2048]{1,0:T(8,128)(2,1)} %param.21) | copy-start | bytes 6291460
  7.2 28.7 %copy-start.4 = (bf16[2048,128]{1,0:T(8,128)(2,1)S(1)}, bf16[2048,128]{1,0:T(8,128)(2,1)}, u32[]{:S(2)}) copy-start(bf16[2048,128]{1,0:T(8,128)(2,1)} %param.19) | copy-start | bytes 1572868
  8.9 35.4 %copy-start.24 = (s32[128]{0:T(128)}, s32[128]{0:T(128)S(1)}, u32[]{:S(2)}) copy-start(s32[128]{0:T(128)S(1)} %fusion.76) | copy-start | bytes 1540
  31.7 12.6 %copy-start.25 = (s32[128]{0:T(128)S(1)}, s32[128]{0:T(128)}, u32[]{:S(2)}) copy-start(s32[128]{0:T(128)} %param.17) | copy-start | bytes 1540
  34.8 23.7 %copy-start.14 = (bf16[128,512]{1,0:T(8,128)(2,1)S(1)}, bf16[128,512]{1,0:T(8,128)(2,1)}, u32[]{:S(2)}) copy-start(bf16[128,512]{1,0:T(8,128)(2,1)} %param.20) | copy-start | bytes 393220
  39.7 17.9 %all-to-all-start.1 = ((bf16[128,4,512]{2,1,0:T(4,128)(2,1)}), bf16[128,4,512]{2,1,0:T(4,128)(2,1)S(1)}, u32[]{:S(2)}, u32[]{:S(2)}) async-start(bf16[128,4,512]{2,1,0:T(4,128)(2,1)} %pad_select_fusion), calls=%async_computation.1 | async-start | bytes 1048576 | tf_op jit(solution)/shard_map/all_to_all | solution.py:147
  44.2 65.4 %all-gather.3.cloned.1.call-start = ((), (), s32[]{:S(2)}) async-start(), calls=%async_computation.4 | async-start | bytes 4456448 | tf_op jit(solution)/shard_map/all_gather | solution.py:23
  44.8 16.3 %copy-start.21 = (pred[128]{0:T(512)(128)(4,1)}, pred[128]{0:T(512)(128)(4,1)S(1)}, u32[]{:S(2)}) copy-start(pred[128]{0:T(512)(128)(4,1)S(1)} %get-tuple-element.602) | copy-start | bytes 388
  58.8 2.2 copy-start.17
  59.5 1.5 copy-start.19
  61.0 53.1 %copy-start.11 = (bf16[128,2048]{1,0:T(8,128)(2,1)}, bf16[128,2048]{1,0:T(8,128)(2,1)S(1)}, u32[]{:S(2)}) copy-start(bf16[128,2048]{1,0:T(8,128)(2,1)S(1)} %get-tuple-element.605) | copy-start | bytes 1572868
  61.1 53.0 %copy-start.6 = (bf16[128,512]{1,0:T(8,128)(2,1)}, bf16[128,512]{1,0:T(8,128)(2,1)S(1)}, u32[]{:S(2)}) copy-start(bf16[128,512]{1,0:T(8,128)(2,1)S(1)} %get-tuple-element.592) | copy-start | bytes 393220
  61.9 134.4 %all-gather.5.cloned.1.call-start = ((), (), s32[]{:S(2)}) async-start(), calls=%async_computation.5 | async-start | bytes 4456448 | tf_op jit(solution)/shard_map/all_gather | solution.py:23
  138.5 197.3 %all-reduce.7.cloned.1.call-start = ((), (), s32[]{:S(2)}) async-start(), calls=%async_computation.6 | async-start | bytes 262144 | tf_op jit(solution)/shard_map/psum | solution.py:13
  209.6 43.0 %copy-start.2 = (f32[128,512]{1,0:T(8,128)S(1)}, f32[128,512]{1,0:T(8,128)}, u32[]{:S(2)}) copy-start(f32[128,512]{1,0:T(8,128)} %copy-done.1) | copy-start | bytes 786436
  209.6 43.0 %copy-start.18 = (f32[128]{0:T(128)S(1)}, f32[128]{0:T(128)}, u32[]{:S(2)}) copy-start(f32[128]{0:T(128)} %copy-done.17) | copy-start | bytes 1540
  209.6 43.0 %copy-start.20 = (f32[128]{0:T(128)S(1)}, f32[128]{0:T(128)}, u32[]{:S(2)}) copy-start(f32[128]{0:T(128)} %copy-done.19) | copy-start | bytes 1540
  211.5 0.7 copy-start.8
  224.5 4.7 copy-start.9
  244.1 4.7 copy-start.9
  248.7 4.8 copy-start.5
  248.7 5.0 copy-start.23
  248.8 7.0 %copy-start.7 = (bf16[128,512]{1,0:T(8,128)(2,1)S(1)}, bf16[128,512]{1,0:T(8,128)(2,1)}, u32[]{:S(2)}) copy-start(bf16[128,512]{1,0:T(8,128)(2,1)} %get-tuple-element.586) | copy-start | bytes 393220
  253.5 84.7 %copy-start.15 = (bf16[128,512]{1,0:T(8,128)(2,1)S(1)}, bf16[128,512]{1,0:T(8,128)(2,1)}, u32[]{:S(2)}) copy-start(bf16[128,512]{1,0:T(8,128)(2,1)} %param.20) | copy-start | bytes 393220
  253.5 85.6 %copy-start.22 = (pred[128]{0:T(512)(128)(4,1)S(1)}, pred[128]{0:T(512)(128)(4,1)}, u32[]{:S(2)}) copy-start(pred[128]{0:T(512)(128)(4,1)} %copy-done.21) | copy-start | bytes 388
  253.7 84.5 %copy-start.3 = (f32[128,512]{1,0:T(8,128)}, f32[128,512]{1,0:T(8,128)S(1)}, u32[]{:S(2)}) copy-start(f32[128,512]{1,0:T(8,128)S(1)} %convert_add_fusion) | copy-start | bytes 786436
  255.7 142.8 %all-reduce.9.cloned.1.call-start = ((), (), s32[]{:S(2)}) async-start(), calls=%async_computation.7 | async-start | bytes 262144 | tf_op jit(solution)/shard_map/psum | solution.py:14
  335.8 221.8 %all-reduce.11.cloned.1.call-start = ((), (), s32[]{:S(2)}) async-start(), calls=%async_computation.8 | async-start | bytes 5242880 | tf_op jit(solution)/shard_map/psum | solution.py:298
  344.2 20.7 %all-to-all-start.2 = ((bf16[128,1,2,512]{3,2,1,0:T(2,128)(2,1)}), bf16[128,1,2,512]{3,2,1,0:T(2,128)(2,1)S(1)}, u32[]{:S(2)}, u32[]{:S(2)}) async-start(bf16[128,1,2,512]{3,2,1,0:T(2,128)(2,1)} %get-tuple-element.590), calls=%async_computation.2 | async-start | bytes 524288 | tf_op jit(solution)/shard_map/all_to_all | solution.py:49
  364.9 35.3 %copy-start.10 = (bf16[128,1,2,512]{3,2,1,0:T(2,128)(2,1)}, bf16[128,1,2,512]{3,2,1,0:T(2,128)(2,1)S(1)}, u32[]{:S(2)}) copy-start(bf16[128,1,2,512]{3,2,1,0:T(2,128)(2,1)S(1)} %all-to-all-done.2) | copy-start | bytes 786436
  364.9 35.3 %all-to-all-start.3 = ((bf16[128,1,2,512]{3,2,1,0:T(2,128)(2,1)}), bf16[128,1,2,512]{3,2,1,0:T(2,128)(2,1)}, u32[]{:S(2)}, u32[]{:S(2)}) async-start(bf16[128,1,2,512]{3,2,1,0:T(2,128)(2,1)} %get-tuple-element.591), calls=%async_computation.3 | async-start | bytes 524288 | tf_op jit(solution)/shard_map/all_to_all | solution.py:49
  557.7 4.2 copy-start.13
  (4 other events, 2.8 us)
Sparse Core Ops, SparseCore 0:
  62.1 47.4 all-gather.2
  138.6 57.7 all-gather.4
  255.9 79.8 all-reduce.6
  338.0 60.5 all-reduce.8
  404.0 153.6 all-reduce.10
